TPU v7x, 32 devices: a whole 2x2x4 slice. The times are simulated.
32 devices in a mesh: samples: 8 (over z, y), variants: 4 (over x, core).
Axes of the slice: x: 2, y: 2, z: 4, core: 2. Of those that a mesh axis runs over, the one named last changes fastest.
Arguments:
- genotypes: int32 [2048, 32768], P('variants', 'samples'), may hold values from 0 to 3, as said below
- weights: float32 [32768], P('samples'), may hold values from 0.25 to 20
Outputs:
- call_mean: float32 [2048], P('variants')
- call_var: float32 [2048], P('variants')
- class_counts: int32 [4, 2048], P(None, 'variants')
- ld_window: float32 [1024, 2048], P('samples', 'variants')
- sample_calls: int32 [2, 32768], P(None, 'samples')
- sample_share: float32 [32768], P('samples')
Inputs may be any that keep to these rules, and one draw needn't show every extreme that they name: `genotypes`: in every variant's row, each aligned group of 8 samples (samples 8 i to 8 i + 7) holds at least one call other than 3.
All inputs are finite; a program needn't handle non-finite values.
Results may differ from a plain program's by a relative error of at most 0.0004.
Values may be sent and summed in bfloat16 or wider, within the bound.
A program may use at most 64 MiB of HBM per device.

v0:
```python
import functools

import jax
import jax.numpy as jnp
from jax import lax
from jax.experimental import pallas as pl
from jax.experimental.pallas import tpu as pltpu
from jax.sharding import PartitionSpec as P

MESH = pl.DeviceIdType.MESH
F32 = jnp.float32
BF16 = jnp.bfloat16
LANES = 128
STEP = 16
SUB = 32
FULL = 32400.0
SLAB = 512


def kernel(
    S,
    V,
    CH,
    gen_hbm,
    w_ref,
    stat_out,
    count_out,
    ld_out,
    call_out,
    share_out,
    gen,
    code,
    ncode,
    scaled,
    nscaled,
    part,
    mine,
    rcv,
    wacc,
    cacc,
    sacc,
    qacc,
    root,
    gat,
    ngat,
    par,
    colm,
    colf,
    cole,
    tall,
    ntall,
    smp,
    gen_sem,
    code_send,
    code_recv,
    stat_send,
    stat_recv,
    par_send,
    par_recv,
    rs_send,
    rs_recv,
    smp_send,
    smp_recv,
):
    s = lax.axis_index("samples")
    v = lax.axis_index("variants")
    rows, width = gen.shape
    R = 2 * rows // S
    H = S // 2
    NC = rows // CH
    blocks = width // LANES
    slabs = width // SLAB
    has_next = v < V - 1
    has_prev = v > 0

    def chunk_rows(c):
        return pl.ds(pl.multiple_of(c * CH, CH), CH)

    def load(k):
        c = lax.rem(k + s, NC)
        return pltpu.make_async_copy(
            gen_hbm.at[chunk_rows(c)], gen.at[chunk_rows(c)], gen_sem.at[c]
        )

    def start_load(k, _):
        load(k).start()
        return 0

    lax.fori_loop(0, NC, start_load, 0)

    barrier = pltpu.get_barrier_semaphore()

    def greet_samples(d, _):
        pl.semaphore_signal(
            barrier,
            inc=1,
            device_id={"samples": lax.rem(s + d, S)},
            device_id_type=MESH,
        )
        return 0

    def greet_variants(d, _):
        pl.semaphore_signal(
            barrier,
            inc=1,
            device_id={"variants": lax.rem(v + d, V)},
            device_id_type=MESH,
        )
        return 0

    lax.fori_loop(1, S, greet_samples, 0)
    lax.fori_loop(1, V, greet_variants, 0)

    root[...] = jnp.sqrt(w_ref[...])
    sacc[...] = jnp.zeros_like(sacc)
    qacc[...] = jnp.zeros_like(qacc)

    def code_copy(c):
        return pltpu.make_async_remote_copy(
            src_ref=code.at[chunk_rows(c)],
            dst_ref=ncode.at[chunk_rows(c)],
            send_sem=code_send.at[c],
            recv_sem=code_recv.at[c],
            device_id={"variants": lax.rem(v + V - 1, V)},
            device_id_type=MESH,
        )

    def piece_copy(c, h):
        here = pl.ds(pl.multiple_of(c * CH + h * SUB, SUB), SUB)
        return pltpu.make_async_remote_copy(
            src_ref=code.at[here],
            dst_ref=ncode.at[here],
            send_sem=code_send.at[c],
            recv_sem=code_recv.at[c],
            device_id={"variants": lax.rem(v + V - 1, V)},
            device_id_type=MESH,
        )

    def first_pass(k, _):
        c = lax.rem(k + s, NC)
        load(k).wait()

        def sixteen(i, _):
            here = pl.ds(pl.multiple_of(c * CH + i * STEP, STEP), STEP)
            zero = jnp.zeros((STEP, LANES), F32)
            w0, w1, w2 = zero, zero, zero
            cnt = jnp.zeros((STEP, LANES), jnp.int32)
            for b in range(blocks):
                lane = slice(b * LANES, (b + 1) * LANES)
                g = gen[here, lane]
                w = jnp.broadcast_to(w_ref[0:1, lane], (STEP, LANES))
                w0 = w0 + jnp.where(g == 0, w, 0.0)
                w1 = w1 + jnp.where(g == 1, w, 0.0)
                w2 = w2 + jnp.where(g == 2, w, 0.0)
                tag = jnp.left_shift(jnp.int32(1), jnp.left_shift(g, 3))
                cnt = cnt + tag
                sacc[:, lane] += tag[:8] + tag[8:]
                code[here, lane] = g.astype(F32).astype(BF16)
            wacc[0, here] = w0
            wacc[1, here] = w1
            wacc[2, here] = w2
            cacc[here] = cnt
            return 0

        def piece(h, _):
            lax.fori_loop(h * (SUB // STEP), (h + 1) * (SUB // STEP), sixteen, 0)

            @pl.when(jnp.logical_and(k == 0, h == 0))
            def _():
                pl.semaphore_wait(barrier, S + V - 2)

            @pl.when(has_prev)
            def _():
                piece_copy(c, h).start()

            return 0

        lax.fori_loop(0, CH // SUB, piece, 0)
        return 0

    lax.fori_loop(0, NC, first_pass, 0)

    def total(x):
        return jnp.sum(x.T, axis=0, keepdims=True)

    cnt = cacc[...]
    lines = [total(wacc[i]) for i in range(3)]
    for level in range(4):
        lines.append(
            total(jnp.bitwise_and(jnp.right_shift(cnt, 8 * level), 255).astype(F32))
        )
    lines.append(jnp.zeros_like(lines[0]))
    gat[s] = jnp.concatenate(lines, axis=0)

    def stat_copy(d, slot):
        return pltpu.make_async_remote_copy(
            src_ref=gat.at[slot],
            dst_ref=gat.at[slot],
            send_sem=stat_send.at[d],
            recv_sem=stat_recv.at[slot],
            device_id={"samples": lax.rem(s + d, S)},
            device_id_type=MESH,
        )

    def send_stat(d, _):
        stat_copy(d, s).start()
        return 0

    lax.fori_loop(1, S, send_stat, 0)

    def wait_stat(d, _):
        stat_copy(d, lax.rem(s + d, S)).wait_recv()
        return 0

    lax.fori_loop(1, S, wait_stat, 0)

    def moments(ref):
        sums = ref[0]
        for t in range(1, S):
            sums = sums + ref[t]
        w0, w1, w2 = sums[0:1], sums[1:2], sums[2:3]
        w_sum = w0 + w1 + w2
        mean = (w1 + 2.0 * w2) / w_sum
        one, two = 1.0 - mean, 2.0 - mean
        var = (w0 * mean * mean + w1 * one * one + w2 * two * two) / w_sum
        factor = 1.0 / jnp.sqrt(w_sum * (var + 1e-05))
        return sums, mean, var, factor

    def norm(ref, t, mean, factor):
        w0, w1, w2 = ref[t, 0:1], ref[t, 1:2], ref[t, 2:3]
        one, two = 1.0 - mean, 2.0 - mean
        length = jnp.sqrt(w0 * mean * mean + w1 * one * one + w2 * two * two)
        return jnp.maximum(length * factor, 1e-12)

    par_copy = pltpu.make_async_remote_copy(
        src_ref=gat,
        dst_ref=ngat,
        send_sem=par_send.at[0],
        recv_sem=par_recv.at[0],
        device_id={"variants": lax.rem(v + V - 1, V)},
        device_id_type=MESH,
    )

    @pl.when(has_prev)
    def _():
        par_copy.start()

    sums, mean, var, factor = moments(gat)
    stat_out[...] = jnp.concatenate([mean, var], axis=0)
    count_out[...] = sums[3:7].astype(jnp.int32)
    level = FULL / norm(gat, s, mean, factor)

    def columns(ref, mean, factor, turned_norms):
        mine_now = FULL / norm(ref, s, mean, factor)
        par[...] = jnp.concatenate(
            [mean, factor, mine_now, jnp.zeros((5, rows), F32)], axis=0
        )
        turned = par[...].T
        colm[...] = jnp.broadcast_to(turned[:, 0:1], colm.shape)
        colf[...] = jnp.broadcast_to(turned[:, 1:2], colf.shape)
        cole[...] = jnp.broadcast_to(turned[:, 2:3], cole.shape)
        every = jnp.concatenate([norm(ref, t, mean, factor) for t in range(S)], axis=0)
        turned_norms[:, 0:S] = every.T

    def scale(src, src_row, dst, dst_row, count, squares):
        def sixteen(i, _):
            here = pl.ds(pl.multiple_of(src_row + i * STEP, STEP), STEP)
            there = pl.ds(pl.multiple_of(dst_row + i * STEP, STEP), STEP)
            m, f = colm[here], colf[here]
            for b in range(blocks):
                lane = slice(b * LANES, (b + 1) * LANES)
                d = src[here, lane].astype(F32)
                r = jnp.broadcast_to(root[0:1, lane], (STEP, LANES))
                x = jnp.where(d < 2.5, r * (d - m) * f, 0.0).astype(BF16)
                dst[there, lane] = x
                if squares:
                    y = x.astype(F32)
                    y = y * y
                    qacc[:, lane] += y[:8] + y[8:]
            return 0

        lax.fori_loop(0, count // STEP, sixteen, 0)

    columns(gat, mean, factor, tall)
    scale(code, 0, scaled, 0, rows, True)

    def rs_copy(owner, slot):
        return pltpu.make_async_remote_copy(
            src_ref=part.at[owner],
            dst_ref=rcv.at[slot],
            send_sem=rs_send.at[owner],
            recv_sem=rs_recv.at[slot],
            device_id={"samples": owner},
            device_id_type=MESH,
        )

    def correlate(left):
        return lax.dot_general(
            left, scaled[...], (((1,), (1,)), ((), ())), preferred_element_type=F32
        )

    level_row = level * (1.0 / FULL)

    def hand_over(value, owner, row):
        e = cole[pl.ds(pl.multiple_of(row, R), R), 0:1]

        @pl.when(owner == s)
        def _():
            mine[...] = value

        @pl.when(owner != s)
        def _():
            q = jnp.round(value * e * level_row)
            q = jnp.clip(q, -32767.0, 32767.0)
            part[owner] = q.astype(jnp.int32).astype(jnp.int16)
            rs_copy(owner, s).start()

    def own_rows(k, _):
        owner = lax.rem(s + k, H)
        rows_here = pl.ds(pl.multiple_of(owner * R, R), R)
        hand_over(correlate(scaled[rows_here, :]), owner, owner * R)

        return 0

    lax.fori_loop(0, H, own_rows, 0)

    packed = sacc[...]
    tags = [
        jnp.bitwise_and(jnp.right_shift(packed, 8 * level), 255).astype(F32)
        for level in range(3)
    ]
    for q, value in enumerate([tags[0] + tags[1] + tags[2], tags[1], qacc[...]]):
        line = jnp.sum(value, axis=0, keepdims=True)
        for i in range(slabs):
            smp[v, pl.ds(q * slabs + i, 1), :] = line[:, i * SLAB : (i + 1) * SLAB]

    def smp_copy(d, slot):
        return pltpu.make_async_remote_copy(
            src_ref=smp.at[slot],
            dst_ref=smp.at[slot],
            send_sem=smp_send.at[d],
            recv_sem=smp_recv.at[slot],
            device_id={"variants": lax.rem(v + d, V)},
            device_id_type=MESH,
        )

    def send_smp(d, _):
        smp_copy(d, v).start()
        return 0

    lax.fori_loop(1, V, send_smp, 0)

    @pl.when(has_next)
    def _():
        par_copy.wait_recv()
        _, nmean, _, nfactor = moments(ngat)
        columns(ngat, nmean, nfactor, ntall)

        def cross(k, _):
            c = lax.rem(k + s, NC)
            code_copy(c).wait_recv()
            scale(ncode, c * CH, nscaled, 0, CH, False)
            got = correlate(nscaled[...])
            for i in range(CH // R):
                owner = H + c * (CH // R) + i
                hand_over(got[i * R : (i + 1) * R], owner, c * CH + i * R)

            return 0

        lax.fori_loop(0, NC, cross, 0)

    def wait_smp(d, _):
        smp_copy(d, lax.rem(v + d, V)).wait_recv()
        return 0

    lax.fori_loop(1, V, wait_smp, 0)
    all_sums = smp[0]
    for t in range(1, V):
        all_sums = all_sums + smp[t]
    call_out[...] = all_sums[: 2 * slabs].astype(jnp.int32)
    share_out[...] = all_sums[2 * slabs :] * F32((width * S) / (rows * V))

    sent_to_me = jnp.logical_or(s < H, has_next)

    def gather(norms, row):
        ld_out[...] = mine[...]
        for t in range(S):

            @pl.when(t != s)
            def _():
                rs_copy(s, t).wait_recv()
                col = norm(gat, t, mean, factor) * (1.0 / FULL)
                e = norms[pl.ds(pl.multiple_of(row, R), R), t : t + 1]
                ld_out[...] += rcv[t].astype(jnp.int32).astype(F32) * e * col

    @pl.when(s < H)
    def _():
        gather(tall, s * R)

    @pl.when(jnp.logical_and(s >= H, has_next))
    def _():
        gather(ntall, (s - H) * R)

    @pl.when(jnp.logical_not(sent_to_me))
    def _():
        ld_out[...] = jnp.zeros_like(ld_out)

    def drain_samples(d, _):
        stat_copy(d, s).wait_send()
        owner = lax.rem(s + d, S)

        @pl.when(jnp.logical_or(owner < H, has_next))
        def _():
            rs_copy(owner, s).wait_send()

        return 0

    lax.fori_loop(1, S, drain_samples, 0)

    def drain_variants(d, _):
        smp_copy(d, v).wait_send()
        return 0

    lax.fori_loop(1, V, drain_variants, 0)

    @pl.when(has_prev)
    def _():
        par_copy.wait_send()

        def drain_codes(c, _):
            code_copy(c).wait_send()
            return 0

        lax.fori_loop(0, NC, drain_codes, 0)


def finish(stats, counts, ld, calls, share, mean, var, counts_o, ld_o, calls_o, share_o):
    slabs = share.shape[0]
    mean[...] = stats[0]
    var[...] = stats[1]
    counts_o[...] = counts[...]
    ld_o[...] = ld[...]
    for i in range(slabs):
        here = slice(i * SLAB, (i + 1) * SLAB)
        for q in range(2):
            calls_o[q : q + 1, here] = calls[q * slabs + i : q * slabs + i + 1]
        share_o[here] = share[i]


def on_device(S, V, genotypes, weights):
    rows, width = genotypes.shape
    R = 2 * rows // S
    CH = max(128, R)
    NC = rows // CH
    slabs = width // SLAB
    vmem = pl.BlockSpec(memory_space=pltpu.VMEM)
    dma = pltpu.SemaphoreType.DMA
    stats, counts, ld, calls, share = pl.pallas_call(
        functools.partial(kernel, S, V, CH),
        out_shape=(
            jax.ShapeDtypeStruct((2, rows), F32),
            jax.ShapeDtypeStruct((4, rows), jnp.int32),
            jax.ShapeDtypeStruct((R, rows), F32),
            jax.ShapeDtypeStruct((2 * slabs, SLAB), jnp.int32),
            jax.ShapeDtypeStruct((slabs, SLAB), F32),
        ),
        in_specs=[pl.BlockSpec(memory_space=pl.ANY), vmem],
        out_specs=(vmem,) * 5,
        scratch_shapes=[
            pltpu.VMEM((rows, width), jnp.int32),
            pltpu.VMEM((rows, width), BF16),
            pltpu.VMEM((rows, width), BF16),
            pltpu.VMEM((rows, width), BF16),
            pltpu.VMEM((CH, width), BF16),
            pltpu.VMEM((S, R, rows), jnp.int16),
            pltpu.VMEM((R, rows), F32),
            pltpu.VMEM((S, R, rows), jnp.int16),
            pltpu.VMEM((3, rows, LANES), F32),
            pltpu.VMEM((rows, LANES), jnp.int32),
            pltpu.VMEM((8, width), jnp.int32),
            pltpu.VMEM((8, width), F32),
            pltpu.VMEM((1, width), F32),
            pltpu.VMEM((S, 8, rows), F32),
            pltpu.VMEM((S, 8, rows), F32),
            pltpu.VMEM((8, rows), F32),
            pltpu.VMEM((rows, LANES), F32),
            pltpu.VMEM((rows, LANES), F32),
            pltpu.VMEM((rows, LANES), F32),
            pltpu.VMEM((rows, LANES), F32),
            pltpu.VMEM((rows, LANES), F32),
            pltpu.VMEM((V, 3 * slabs, SLAB), F32),
            dma((NC,)),
            dma((NC,)),
            dma((NC,)),
            dma((S,)),
            dma((S,)),
            dma((1,)),
            dma((1,)),
            dma((S,)),
            dma((S,)),
            dma((V,)),
            dma((V,)),
        ],
        compiler_params=pltpu.CompilerParams(
            collective_id=0, has_side_effects=True, vmem_limit_bytes=60 * 1024 * 1024
        ),
        name="window_stats",
    )(genotypes, weights.reshape(1, width))
    return pl.pallas_call(
        finish,
        out_shape=(
            jax.ShapeDtypeStruct((rows,), F32),
            jax.ShapeDtypeStruct((rows,), F32),
            jax.ShapeDtypeStruct((4, rows), jnp.int32),
            jax.ShapeDtypeStruct((R, rows), F32),
            jax.ShapeDtypeStruct((2, width), jnp.int32),
            jax.ShapeDtypeStruct((width,), F32),
        ),
        in_specs=[vmem] * 5,
        out_specs=(vmem,) * 6,
        name="finish",
    )(stats, counts, ld, calls, share)


def solution(mesh):
    body = functools.partial(on_device, mesh.shape["samples"], mesh.shape["variants"])
    return jax.shard_map(
        body,
        mesh=mesh,
        in_specs=(P("variants", "samples"), P("samples")),
        out_specs=(
            P("variants"),
            P("variants"),
            P(None, "variants"),
            P("samples", "variants"),
            P(None, "samples"),
            P("samples"),
        ),
        check_vma=False,
    )
```

profile of v0, /device:TPU:21, one launch (start us, length us, event | category | flops | bytes accessed | tf_op | source)
XLA Modules:
  0.0 73.9 jit_solution(16150237757611118358)
XLA Ops:
  0.6 71.6 %window_stats.1 = (f32[2,512]{1,0:T(2,128)}, s32[4,512]{1,0:T(4,128)}, f32[128,512]{1,0:T(8,128)}, s32[16,512]{1,0:T(8,128)}, f32[8,512]{1,0:T(8,128)}) custom-call(s32[512,4096]{1,0:T(8,128)} %gen_hbm.1, f32[1,4096]{1,0:T(1,128)} %bitcast.1), custom_call_target="tpu_custom_call" | custom-call | tf_op jit(solution)/shard_map/window_stats/pallas_call | solution.py:458
  72.2 1.7 %finish.1 = (f32[512]{0:T(512)}, f32[512]{0:T(512)}, s32[4,512]{1,0:T(4,128)}, f32[128,512]{1,0:T(8,128)}, s32[2,4096]{1,0:T(2,128)}, /*index=5*/f32[4096]{0:T(1024)}) custom-call(f32[2,512]{1,0:T(2,128)} %get-tuple-element.11.stats, s32[4,512]{1,0:T(4,128)} %get-tuple-element.12.counts, f32[128,512]{1,0:T(8,128)} %get-tuple-element.13.ld, ...), custom_call_target="tpu_custom_call" | custom-call | tf_op jit(solution)/shard_map/finish/pallas_call | solution.py:509
where the time goes:
time: 74.2 us; the launch traced here: 73.9 us
  Pallas kernels  73.3 us (99%)
    pallas_call x1, Pallas kernels, on_device(): pl.pallas_call(functools.partial(kernel, S, V, CH), out_shape=(jax.ShapeD...  71.6 us
    pallas_call x1, Pallas kernels, on_device(): pl.pallas_call(finish, out_shape=(jax.ShapeDtypeStruct((rows,), F32), jax...  1.74 us

commit v1 on v0

v1 whole, which is shorter than its diff:
```python
import functools

import jax
import jax.numpy as jnp
from jax import lax
from jax.experimental import pallas as pl
from jax.experimental.pallas import tpu as pltpu
from jax.sharding import PartitionSpec as P

MESH = pl.DeviceIdType.MESH
F32 = jnp.float32
BF16 = jnp.bfloat16
LANES = 128
STEP = 16
SUB = 32
FULL = 32400.0
SLAB = 512
EARLY = 7
LEFT = 16


def aligned(x, n):
    return pl.multiple_of(x, n)


def kernel(
    S,
    V,
    gen_hbm,
    w_ref,
    stat_out,
    count_out,
    ld_out,
    call_out,
    share_out,
    gen,
    code,
    ncode,
    pcode,
    scaled,
    other,
    keep_o,
    keep_x,
    ypart_o,
    yrcv_o,
    ypart_n,
    yrcv_n,
    ypart_p,
    yrcv_p,
    zpart_o,
    zpart_n,
    zpart_p,
    zrcv,
    zrcv_p,
    wacc,
    cacc,
    sacc,
    qacc,
    root,
    gat,
    par,
    npar,
    ppar,
    aux,
    col_o,
    col_x,
    lane_o,
    lane_x,
    lane_q,
    tall,
    spread,
    smp_mine,
    smp_mate,
    smp_all,
    gen_sem,
    ncode_send,
    ncode_recv,
    pcode_send,
    pcode_recv,
    stat_send,
    stat_recv,
    par_send,
    par_recv,
    yo_send,
    yo_recv,
    yn_send,
    yn_recv,
    yp_send,
    yp_recv,
    zo_send,
    zn_send,
    zp_send,
    z_recv,
    zp_recv,
    mate_send,
    mate_recv,
    smp_send,
    smp_recv,
):
    s = lax.axis_index("samples")
    v = lax.axis_index("variants")
    rows, width = gen.shape
    R = 2 * rows // S
    H = S // 2
    Q = H // 2
    PAIRS = S // 2
    NP = rows // SUB
    UNIT = min(R, 64)
    NCP = rows // LANES
    KL = width * LEFT // 32 // LANES * LANES
    C = V // 2
    blocks = width // LANES
    slabs = width // SLAB

    pair = lax.div(s, 2)
    y = s - 2 * pair
    mate = s + 1 - 2 * y
    chip = lax.div(v, 2)
    odd = v - 2 * chip == 1
    even = jnp.logical_not(odd)
    near = 2 * chip < C
    far = jnp.logical_not(near)
    has_next = v < V - 1
    has_prev = v > 0
    next_part = jnp.logical_and(odd, has_next)
    next_full = jnp.logical_and(even, near)
    prev_part = jnp.logical_and(even, has_prev)
    prev_full = jnp.logical_and(odd, far)
    send_down_full = jnp.logical_and(odd, near)
    send_down_part = prev_part
    send_up_full = jnp.logical_and(even, far)
    send_up_part = next_part
    from_next = jnp.logical_or(next_part, next_full)
    from_prev = jnp.logical_or(send_up_full, send_up_part)
    does_prev = jnp.logical_or(prev_part, prev_full)
    down = lax.rem(v + V - 1, V)
    up = lax.rem(v + 1, V)
    turn = lax.div(lax.div(pair * NP, PAIRS), 4) * 4

    def piece_rows(i):
        return pl.ds(aligned(lax.rem(i + turn, NP) * SUB, SUB), SUB)

    def load(i):
        return pltpu.make_async_copy(
            gen_hbm.at[piece_rows(i)], gen.at[piece_rows(i)], gen_sem.at[i]
        )

    def loop(start, stop, body):
        def step(i, _):
            body(i)
            return 0

        lax.fori_loop(start, stop, step, 0)

    loop(0, NP, lambda i: load(i).start())

    barrier = pltpu.get_barrier_semaphore()

    def greet(device):
        pl.semaphore_signal(barrier, inc=1, device_id=device, device_id_type=MESH)

    loop(1, S, lambda d: greet({"samples": lax.rem(s + d, S)}))
    loop(1, V, lambda d: greet({"variants": lax.rem(v + d, V)}))

    def cross_greet(d):
        there = 2 * lax.rem(pair + d, PAIRS) + y

        @pl.when(has_prev)
        def _():
            greet({"samples": there, "variants": down})

        @pl.when(has_next)
        def _():
            greet({"samples": there, "variants": up})

    loop(1, PAIRS, cross_greet)
    greetings = (
        S
        + V
        - 2
        + (PAIRS - 1) * (has_prev.astype(jnp.int32) + has_next.astype(jnp.int32))
    )

    root[...] = jnp.sqrt(w_ref[...])
    sacc[...] = jnp.zeros_like(sacc)
    qacc[...] = jnp.zeros_like(qacc)

    def piece_copy(i, buf, send, recv, device, lo, hi):
        here = piece_rows(i)
        return pltpu.make_async_remote_copy(
            src_ref=code.at[here, lo:hi],
            dst_ref=buf.at[here, lo:hi],
            send_sem=send.at[i],
            recv_sem=recv.at[i],
            device_id={"variants": device},
            device_id_type=MESH,
        )

    def down_copy(i, hi):
        return piece_copy(i, ncode, ncode_send, ncode_recv, down, 0, hi)

    def up_copy(i, lo):
        return piece_copy(i, pcode, pcode_send, pcode_recv, up, lo, width)

    def send_far(i):
        @pl.when(send_down_part)
        def _():
            down_copy(i, KL).start()

        @pl.when(send_up_part)
        def _():
            up_copy(i, KL).start()

    def first_pass(k):
        load(k).wait()
        base = lax.rem(k + turn, NP) * SUB

        def sixteen(i):
            here = pl.ds(aligned(base + i * STEP, STEP), STEP)
            zero = jnp.zeros((STEP, LANES), F32)
            w0, w1, w2 = zero, zero, zero
            cnt = jnp.zeros((STEP, LANES), jnp.int32)
            for b in range(blocks):
                lane = slice(b * LANES, (b + 1) * LANES)
                g = gen[here, lane]
                w = jnp.broadcast_to(w_ref[0:1, lane], (STEP, LANES))
                w0 = w0 + jnp.where(g == 0, w, 0.0)
                w1 = w1 + jnp.where(g == 1, w, 0.0)
                w2 = w2 + jnp.where(g == 2, w, 0.0)
                tag = jnp.left_shift(jnp.int32(1), jnp.left_shift(g, 3))
                cnt = cnt + tag
                sacc[:, lane] += tag[:8] + tag[8:]
                code[here, lane] = g.astype(F32).astype(BF16)
            wacc[0, here] = w0
            wacc[1, here] = w1
            wacc[2, here] = w2
            cacc[here] = cnt

        loop(0, SUB // STEP, sixteen)

        @pl.when(k == 0)
        def _():
            pl.semaphore_wait(barrier, greetings)

        @pl.when(send_down_full)
        def _():
            down_copy(k, width).start()

        @pl.when(send_up_full)
        def _():
            up_copy(k, 0).start()

        @pl.when(k < EARLY)
        def _():
            send_far(k)

    loop(0, NP, first_pass)

    def total(x):
        return jnp.sum(x.T, axis=0, keepdims=True)

    cnt = cacc[...]
    lines = [total(wacc[i]) for i in range(3)]
    for level in range(4):
        lines.append(
            total(jnp.bitwise_and(jnp.right_shift(cnt, 8 * level), 255).astype(F32))
        )
    lines.append(jnp.zeros_like(lines[0]))
    gat[s] = jnp.concatenate(lines, axis=0)

    def stat_copy(d, slot):
        return pltpu.make_async_remote_copy(
            src_ref=gat.at[slot],
            dst_ref=gat.at[slot],
            send_sem=stat_send.at[d],
            recv_sem=stat_recv.at[slot],
            device_id={"samples": lax.rem(s + d, S)},
            device_id_type=MESH,
        )

    loop(1, S, lambda d: stat_copy(d, s).start())
    loop(1, S, lambda d: stat_copy(d, lax.rem(s + d, S)).wait_recv())

    sums = gat[0]
    for t in range(1, S):
        sums = sums + gat[t]
    w0, w1, w2 = sums[0:1], sums[1:2], sums[2:3]
    w_sum = w0 + w1 + w2
    mean = (w1 + 2.0 * w2) / w_sum
    one, two = 1.0 - mean, 2.0 - mean
    ms, os, ts = mean * mean, one * one, two * two
    var = (w0 * ms + w1 * os + w2 * ts) / w_sum
    factor = 1.0 / jnp.sqrt(w_sum * (var + 1e-05))
    par[0:1] = mean
    par[1:2] = factor
    for t in range(S):
        length = jnp.sqrt(gat[t, 0:1] * ms + gat[t, 1:2] * os + gat[t, 2:3] * ts)
        par[2 + t : 3 + t] = jnp.maximum(length * factor, 1e-12)
    spare = par.shape[0] - 2 - S
    if spare:
        par[2 + S :] = jnp.zeros((spare, rows), F32)

    def par_copy(i, dst, device):
        return pltpu.make_async_remote_copy(
            src_ref=par,
            dst_ref=dst,
            send_sem=par_send.at[i],
            recv_sem=par_recv.at[i],
            device_id={"variants": device},
            device_id_type=MESH,
        )

    @pl.when(has_prev)
    def _():
        par_copy(0, npar, down).start()

    @pl.when(from_prev)
    def _():
        par_copy(1, ppar, up).start()

    loop(EARLY, NP, send_far)

    stat_out[...] = jnp.concatenate([mean, var], axis=0)
    count_out[...] = sums[3:7].astype(jnp.int32)

    def build(src, col, lane):
        def of(who):
            line = jnp.zeros((1, rows), F32)
            for t in range(S):
                line = line + src[2 + t : 3 + t] * (who == t).astype(F32)
            return line

        mine, its = of(s), of(mate)
        both = jnp.sqrt(mine * mine + its * its)
        aux[...] = jnp.concatenate(
            [src[0:2], FULL / mine, its, FULL / both, jnp.zeros((3, rows), F32)],
            axis=0,
        )
        turned = aux[...].T
        for i in range(5):
            col[i] = jnp.broadcast_to(turned[:, i : i + 1], (rows, LANES))
        lane[0:1] = 1.0 / mine
        lane[1:2] = its * (1.0 / FULL)
        lane[2:3] = 1.0 / both
        sizes = []
        for q in range(PAIRS):
            a, b = src[2 + 2 * q : 3 + 2 * q], src[3 + 2 * q : 4 + 2 * q]
            sizes.append(jnp.sqrt(a * a + b * b))
        left = -PAIRS % 8
        if left:
            sizes.append(jnp.zeros((left, rows), F32))
        tall[:, 0 : PAIRS + left] = jnp.concatenate(sizes, axis=0).T

    def scale(src, src_row, dst, dst_row, count, lo, hi, col, squares):
        def sixteen(i):
            here = pl.ds(aligned(src_row + i * STEP, STEP), STEP)
            there = pl.ds(aligned(dst_row + i * STEP, STEP), STEP)
            m, f = col[0, here], col[1, here]
            for b in range(lo // LANES, hi // LANES):
                lane = slice(b * LANES, (b + 1) * LANES)
                d = src[here, lane].astype(F32)
                r = jnp.broadcast_to(root[0:1, lane], (STEP, LANES))
                x = jnp.where(d < 2.5, r * (d - m) * f, 0.0).astype(BF16)
                dst[there, lane] = x
                if squares:
                    yy = x.astype(F32)
                    yy = yy * yy
                    qacc[:, lane] += yy[:8] + yy[8:]

        loop(0, count // STEP, sixteen)

    def rows_of():
        row = lax.rem(s, H) * R
        for q in range(PAIRS):
            spread[q] = jnp.broadcast_to(
                tall[pl.ds(aligned(row, R), R), q : q + 1], (R, LANES)
            )

    build(par, col_o, lane_o)
    for q in range(PAIRS):
        lane_q[q] = jnp.sqrt(
            par[2 + 2 * q : 3 + 2 * q] ** 2 + par[3 + 2 * q : 4 + 2 * q] ** 2
        ) * (1.0 / FULL)

    @pl.when(s < H)
    def _():
        rows_of()

    scale(code, 0, scaled, 0, rows, 0, width, col_o, True)

    def dot(a, b):
        return lax.dot_general(
            a, b, (((1,), (1,)), ((), ())), preferred_element_type=F32
        )

    def coded(value, e, line):
        q = jnp.round(value * e * line)
        q = jnp.clip(q, -32767.0, 32767.0)
        return q.astype(jnp.int32).astype(jnp.int16)

    def pack(src, src_row, col, col_row, lane, lane_at, cols, count, dst, dst_row):
        def sixteen(i):
            here = pl.ds(aligned(src_row + i * STEP, STEP), STEP)
            e = col[2, pl.ds(aligned(col_row + i * STEP, STEP), STEP)]
            for b in range(cols // LANES):
                part = slice(b * LANES, (b + 1) * LANES)
                line = lane[0:1, pl.ds(aligned(lane_at + b * LANES, LANES), LANES)]
                dst[pl.ds(aligned(dst_row + i * STEP, STEP), STEP), part] = coded(
                    src[here, part], e, line
                )

        loop(0, count // STEP, sixteen)

    def merge(
        src,
        src_row,
        got,
        got_row,
        col,
        col_row,
        lane,
        lane_at,
        cols,
        count,
        dst,
        dst_row,
        final,
    ):
        def sixteen(i):
            here = pl.ds(aligned(src_row + i * STEP, STEP), STEP)
            line_rows = pl.ds(aligned(col_row + i * STEP, STEP), STEP)
            there = pl.ds(aligned(dst_row + i * STEP, STEP), STEP)
            theirs = pl.ds(aligned(got_row + i * STEP, STEP), STEP)
            d, e = col[3, line_rows], col[4, line_rows]
            for b in range(cols // LANES):
                part = slice(b * LANES, (b + 1) * LANES)
                lanes = pl.ds(aligned(lane_at + b * LANES, LANES), LANES)
                q = got[theirs, part].astype(jnp.int32).astype(F32)
                value = src[here, part] + q * d * lane[1:2, lanes]
                if final:
                    dst[there, part] = value
                else:
                    dst[there, part] = coded(value, e, lane[2:3, lanes])

        loop(0, count // STEP, sixteen)

    def copy_to(src, dst, send, recv, device):
        return pltpu.make_async_remote_copy(
            src_ref=src,
            dst_ref=dst,
            send_sem=send,
            recv_sem=recv,
            device_id=device,
            device_id_type=MESH,
        )

    def yo_copy(j):
        return copy_to(
            ypart_o.at[j], yrcv_o.at[j], yo_send.at[j], yo_recv.at[j], {"samples": mate}
        )

    def zo_copy(j):
        return copy_to(
            zpart_o.at[j],
            zrcv.at[pair],
            zo_send.at[j],
            z_recv.at[pair],
            {"samples": 2 * j + y},
        )

    def own_dot(o):
        here = pl.ds(aligned(o * R, R), R)
        keep_o[here, :] = dot(scaled[here, :], scaled[...])

    def own_rows(k):
        give = k < Q
        j = lax.rem(lax.rem(k, Q) + pair, Q)
        o = 2 * j + jnp.where(give, 1 - y, y)
        own_dot(o)

        @pl.when(give)
        def _():
            pack(
                keep_o, o * R, col_o, o * R, lane_o, 0, rows, R, ypart_o.at[j], 0
            )
            yo_copy(j).start()

    loop(0, H, own_rows)

    packed = sacc[...]
    tags = [
        jnp.bitwise_and(jnp.right_shift(packed, 8 * level), 255).astype(F32)
        for level in range(3)
    ]
    for q, value in enumerate([tags[0] + tags[1] + tags[2], tags[1], qacc[...]]):
        line = jnp.sum(value, axis=0, keepdims=True)
        for i in range(slabs):
            at = q * slabs + i
            smp_mine[at : at + 1, :] = line[:, i * SLAB : (i + 1) * SLAB]

    mate_copy = copy_to(
        smp_mine,
        smp_mate,
        mate_send.at[0],
        mate_recv.at[0],
        {"variants": v + 1 - 2 * (v - 2 * chip)},
    )
    mate_copy.start()

    def collect_own(k):
        j = lax.rem(k + pair, Q)
        o = 2 * j + y
        yo_copy(j).wait_recv()
        args = (keep_o, o * R, yrcv_o.at[j], 0, col_o, o * R, lane_o, 0, rows, R)

        @pl.when(o == s)
        def _():
            merge(*args, ld_out, 0, True)

        @pl.when(o != s)
        def _():
            merge(*args, zpart_o.at[j], 0, False)
            zo_copy(j).start()

    def yn_copy(at, size):
        j = lax.div(lax.div(at, R), 2)
        here = pl.ds(aligned(at - lax.div(at, R) * R, size), size)
        unit = lax.div(at, UNIT)
        return copy_to(
            ypart_n.at[j, here],
            yrcv_n.at[j, here],
            yn_send.at[unit],
            yn_recv.at[unit],
            {"samples": mate},
        )

    def zn_copy(at, size):
        r = lax.div(at, R)
        here = pl.ds(aligned(at - r * R, size), size)
        return copy_to(
            zpart_n.at[lax.div(r, 2), here],
            zrcv.at[pair, here],
            zn_send.at[lax.div(at, UNIT)],
            z_recv.at[pair],
            {"samples": H + r},
        )

    def next_rows(k, size):
        return lax.rem(k * size + turn * SUB, rows)

    def next_parity(at):
        r = lax.div(at, R)
        return r - 2 * lax.div(r, 2) == y

    def collect_next(k, size):
        at = next_rows(k, size)
        r = lax.div(at, R)

        @pl.when(next_parity(at))
        def _():
            yn_copy(at, size).wait_recv()
            j = lax.div(r, 2)
            off = at - r * R
            args = (keep_x, at, yrcv_n.at[j], off, col_x, at, lane_o, 0, rows, size)

            @pl.when(H + r == s)
            def _():
                merge(*args, ld_out, off, True)

            @pl.when(H + r != s)
            def _():
                merge(*args, zpart_n.at[j], off, False)
                zn_copy(at, size).start()

    def next_role(size, hi):
        per = size // SUB

        def chunk(k):
            at = next_rows(k, size)
            for i in range(per):
                down_copy(k * per + i, hi).wait_recv()
            scale(ncode, at, other, 0, size, 0, hi, col_x, False)
            here = pl.ds(aligned(at, size), size)
            keep_x[here, :] = dot(other[0:size, 0:hi], scaled[:, 0:hi])
            r = lax.div(at, R)

            @pl.when(jnp.logical_not(next_parity(at)))
            def _():
                pack(
                    keep_x,
                    at,
                    col_x,
                    at,
                    lane_o,
                    0,
                    rows,
                    size,
                    ypart_n.at[lax.div(r, 2)],
                    at - r * R,
                )
                yn_copy(at, size).start()

            @pl.when(k > 0)
            def _():
                collect_next(k - 1, size)

        loop(0, rows // size, chunk)
        collect_next(rows // size - 1, size)

    def yp_copy(c):
        return copy_to(
            ypart_p.at[c], yrcv_p.at[c], yp_send.at[c], yp_recv.at[c], {"samples": mate}
        )

    def zp_copy(j, c):
        return copy_to(
            zpart_p.at[j, c],
            zrcv_p.at[pair, c],
            zp_send.at[j],
            zp_recv.at[pair],
            {"samples": H + 2 * j + y, "variants": down},
        )

    def prev_chunk(k):
        return lax.rem(k + lax.div(turn * SUB, LANES), NCP)

    def collect_prev(k):
        c = prev_chunk(k)
        yp_copy(c).wait_recv()

        def one(i):
            j = lax.rem(i + pair, Q)
            o = (2 * j + y) * R
            merge(
                keep_x,
                c * rows + o,
                yrcv_p.at[c, j],
                0,
                col_o,
                o,
                lane_x,
                c * LANES,
                LANES,
                R,
                zpart_p.at[j, c],
                0,
                False,
            )
            zp_copy(j, c).start()

        loop(0, Q, one)

    def prev_role(lo):
        per = LANES // SUB

        def chunk(k):
            c = prev_chunk(k)
            for i in range(per):
                up_copy(k * per + i, lo).wait_recv()
            scale(pcode, c * LANES, other, 0, LANES, lo, width, col_x, False)
            here = pl.ds(aligned(c * rows, rows), rows)
            keep_x[here, 0:LANES] = dot(scaled[:, lo:width], other[0:LANES, lo:width])

            def one(j):
                o = (2 * j + 1 - y) * R
                pack(
                    keep_x,
                    c * rows + o,
                    col_o,
                    o,
                    lane_x,
                    c * LANES,
                    LANES,
                    R,
                    ypart_p.at[c, j],
                    0,
                )

            loop(0, Q, one)
            yp_copy(c).start()

            @pl.when(k > 0)
            def _():
                collect_prev(k - 1)

        loop(0, NCP, chunk)
        collect_prev(NCP - 1)

    def with_next():
        par_copy(0, npar, down).wait_recv()
        build(npar, col_x, lane_x)

        @pl.when(s >= H)
        def _():
            rows_of()


    def with_prev():
        par_copy(1, ppar, up).wait_recv()
        build(ppar, col_x, lane_x)

    @pl.when(prev_full)
    def _():
        with_prev()
        prev_role(0)

    @pl.when(next_full)
    def _():
        with_next()
        next_role(R, width)

    loop(0, Q, collect_own)

    mate_copy.wait_recv()
    smp_all[chip] = smp_mine[...] + smp_mate[...]

    def smp_copy(d, slot):
        return copy_to(
            smp_all.at[slot],
            smp_all.at[slot],
            smp_send.at[d],
            smp_recv.at[slot],
            {"variants": lax.rem(v + 2 * d, V)},
        )

    loop(1, C, lambda d: smp_copy(d, chip).start())

    @pl.when(prev_part)
    def _():
        with_prev()
        prev_role(KL)

    @pl.when(next_part)
    def _():
        with_next()
        next_role(UNIT, KL)

    @pl.when(jnp.logical_and(jnp.logical_not(from_next), has_next))
    def _():
        with_next()

    loop(1, C, lambda d: smp_copy(d, lax.rem(chip + d, C)).wait_recv())
    all_sums = smp_all[0]
    for t in range(1, C):
        all_sums = all_sums + smp_all[t]
    call_out[...] = all_sums[: 2 * slabs].astype(jnp.int32)
    share_out[...] = all_sums[2 * slabs :] * F32((width * S) / (rows * V))

    def gather(got, q, part, wide):
        def sixteen(i):
            here = pl.ds(aligned(i * STEP, STEP), STEP)
            e = spread[q, here]
            for b in range(rows // LANES):
                lanes = slice(b * LANES, (b + 1) * LANES)
                line = lane_q[q, 0:1, lanes]
                piece = got[b, here] if wide else got[here, lanes]
                ld_out[here, lanes] += piece.astype(jnp.int32).astype(F32) * e * line

        loop(0, R // STEP, sixteen)

    def gather_pairs(d):
        q = lax.rem(pair + d, PAIRS)
        copy_to(
            zrcv.at[q], zrcv.at[q], zo_send.at[0], z_recv.at[q], {"samples": mate}
        ).wait_recv()
        gather(zrcv.at[q], q, None, False)

    def gather_prev(d):
        q = lax.rem(pair + d, PAIRS)
        copy_to(
            zrcv_p.at[q], zrcv_p.at[q], zp_send.at[0], zp_recv.at[q], {"samples": mate}
        ).wait_recv()
        gather(zrcv_p.at[q], q, None, True)

    @pl.when(s < H)
    def _():
        loop(1, PAIRS, gather_pairs)

    @pl.when(s >= H)
    def _():
        @pl.when(from_next)
        def _():
            loop(1, PAIRS, gather_pairs)

        @pl.when(jnp.logical_not(from_next))
        def _():
            ld_out[...] = jnp.zeros_like(ld_out)

        @pl.when(from_prev)
        def _():
            loop(0, PAIRS, gather_prev)

    loop(1, S, lambda d: stat_copy(d, s).wait_send())
    loop(1, C, lambda d: smp_copy(d, chip).wait_send())
    mate_copy.wait_send()

    def drain_own(j):
        yo_copy(j).wait_send()

        @pl.when(2 * j + y != s)
        def _():
            zo_copy(j).wait_send()

    loop(0, Q, drain_own)

    def drain_next(size):
        def one(k):
            at = next_rows(k, size)
            r = lax.div(at, R)
            mine = next_parity(at)

            @pl.when(jnp.logical_not(mine))
            def _():
                yn_copy(at, size).wait_send()

            @pl.when(jnp.logical_and(mine, H + r != s))
            def _():
                zn_copy(at, size).wait_send()

        loop(0, rows // size, one)

    @pl.when(next_full)
    def _():
        drain_next(R)

    @pl.when(next_part)
    def _():
        drain_next(UNIT)

    @pl.when(does_prev)
    def _():
        loop(0, NCP, lambda c: yp_copy(c).wait_send())

        def drain(j):
            copy_to(
                zpart_p.at[j], zpart_p.at[j], zp_send.at[j], zp_recv.at[0], {"samples": mate}
            ).wait_send()

        loop(0, Q, drain)

    @pl.when(has_prev)
    def _():
        par_copy(0, npar, down).wait_send()

    @pl.when(from_prev)
    def _():
        par_copy(1, ppar, up).wait_send()

    @pl.when(send_down_full)
    def _():
        loop(0, NP, lambda i: down_copy(i, width).wait_send())

    @pl.when(send_down_part)
    def _():
        loop(0, NP, lambda i: down_copy(i, KL).wait_send())

    @pl.when(send_up_full)
    def _():
        loop(0, NP, lambda i: up_copy(i, 0).wait_send())

    @pl.when(send_up_part)
    def _():
        loop(0, NP, lambda i: up_copy(i, KL).wait_send())


def finish(stats, counts, ld, calls, share, mean, var, counts_o, ld_o, calls_o, share_o):
    slabs = share.shape[0]
    mean[...] = stats[0]
    var[...] = stats[1]
    counts_o[...] = counts[...]
    ld_o[...] = ld[...]
    for i in range(slabs):
        here = slice(i * SLAB, (i + 1) * SLAB)
        for q in range(2):
            calls_o[q : q + 1, here] = calls[q * slabs + i : q * slabs + i + 1]
        share_o[here] = share[i]


def on_device(S, V, genotypes, weights):
    rows, width = genotypes.shape
    R = 2 * rows // S
    H = S // 2
    Q = H // 2
    PAIRS = S // 2
    C = V // 2
    NP = rows // SUB
    NCP = rows // LANES
    units = rows // min(R, 64)
    lines = -(-(2 + S) // 8) * 8
    slabs = width // SLAB
    vmem = pl.BlockSpec(memory_space=pltpu.VMEM)
    dma = pltpu.SemaphoreType.DMA
    stats, counts, ld, calls, share = pl.pallas_call(
        functools.partial(kernel, S, V),
        out_shape=(
            jax.ShapeDtypeStruct((2, rows), F32),
            jax.ShapeDtypeStruct((4, rows), jnp.int32),
            jax.ShapeDtypeStruct((R, rows), F32),
            jax.ShapeDtypeStruct((2 * slabs, SLAB), jnp.int32),
            jax.ShapeDtypeStruct((slabs, SLAB), F32),
        ),
        in_specs=[pl.BlockSpec(memory_space=pl.ANY), vmem],
        out_specs=(vmem,) * 5,
        scratch_shapes=[
            pltpu.VMEM((rows, width), jnp.int32),
            pltpu.VMEM((rows, width), BF16),
            pltpu.VMEM((rows, width), BF16),
            pltpu.VMEM((rows, width), BF16),
            pltpu.VMEM((rows, width), BF16),
            pltpu.VMEM((max(R, LANES), width), BF16),
            pltpu.VMEM((rows, rows), F32),
            pltpu.VMEM((NCP * rows, rows), F32),
            pltpu.VMEM((Q, R, rows), jnp.int16),
            pltpu.VMEM((Q, R, rows), jnp.int16),
            pltpu.VMEM((Q, R, rows), jnp.int16),
            pltpu.VMEM((Q, R, rows), jnp.int16),
            pltpu.VMEM((NCP, Q, R, LANES), jnp.int16),
            pltpu.VMEM((NCP, Q, R, LANES), jnp.int16),
            pltpu.VMEM((Q, R, rows), jnp.int16),
            pltpu.VMEM((Q, R, rows), jnp.int16),
            pltpu.VMEM((Q, NCP, R, LANES), jnp.int16),
            pltpu.VMEM((PAIRS, R, rows), jnp.int16),
            pltpu.VMEM((PAIRS, NCP, R, LANES), jnp.int16),
            pltpu.VMEM((3, rows, LANES), F32),
            pltpu.VMEM((rows, LANES), jnp.int32),
            pltpu.VMEM((8, width), jnp.int32),
            pltpu.VMEM((8, width), F32),
            pltpu.VMEM((1, width), F32),
            pltpu.VMEM((S, 8, rows), F32),
            pltpu.VMEM((lines, rows), F32),
            pltpu.VMEM((lines, rows), F32),
            pltpu.VMEM((lines, rows), F32),
            pltpu.VMEM((8, rows), F32),
            pltpu.VMEM((5, rows, LANES), F32),
            pltpu.VMEM((5, rows, LANES), F32),
            pltpu.VMEM((8, rows), F32),
            pltpu.VMEM((8, rows), F32),
            pltpu.VMEM((PAIRS, 1, rows), F32),
            pltpu.VMEM((rows, LANES), F32),
            pltpu.VMEM((PAIRS, R, LANES), F32),
            pltpu.VMEM((3 * slabs, SLAB), F32),
            pltpu.VMEM((3 * slabs, SLAB), F32),
            pltpu.VMEM((C, 3 * slabs, SLAB), F32),
            dma((NP,)),
            dma((NP,)),
            dma((NP,)),
            dma((NP,)),
            dma((NP,)),
            dma((S,)),
            dma((S,)),
            dma((2,)),
            dma((2,)),
            dma((Q,)),
            dma((Q,)),
            dma((units,)),
            dma((units,)),
            dma((NCP,)),
            dma((NCP,)),
            dma((Q,)),
            dma((units,)),
            dma((Q,)),
            dma((PAIRS,)),
            dma((PAIRS,)),
            dma((1,)),
            dma((1,)),
            dma((C,)),
            dma((C,)),
        ],
        compiler_params=pltpu.CompilerParams(
            collective_id=0, has_side_effects=True, vmem_limit_bytes=60 * 1024 * 1024
        ),
        name="window_stats",
    )(genotypes, weights.reshape(1, width))
    return pl.pallas_call(
        finish,
        out_shape=(
            jax.ShapeDtypeStruct((rows,), F32),
            jax.ShapeDtypeStruct((rows,), F32),
            jax.ShapeDtypeStruct((4, rows), jnp.int32),
            jax.ShapeDtypeStruct((R, rows), F32),
            jax.ShapeDtypeStruct((2, width), jnp.int32),
            jax.ShapeDtypeStruct((width,), F32),
        ),
        in_specs=[vmem] * 5,
        out_specs=(vmem,) * 6,
        name="finish",
    )(stats, counts, ld, calls, share)


def solution(mesh):
    body = functools.partial(on_device, mesh.shape["samples"], mesh.shape["variants"])
    return jax.shard_map(
        body,
        mesh=mesh,
        in_specs=(P("variants", "samples"), P("samples")),
        out_specs=(
            P("variants"),
            P("variants"),
            P(None, "variants"),
            P("samples", "variants"),
            P(None, "samples"),
            P("samples"),
        ),
        check_vma=False,
    )
```

time: 74.2 us -> 54.6 us (0.74)
  the two profiles are of different devices: /device:TPU:21 before, /device:TPU:0 now
where the time goes in v1:
time: 54.6 us; the launch traced here: 54.4 us
  Pallas kernels  53.8 us (99%)
  between operations  0.64 us (1%)
    pallas_call x1, Pallas kernels, on_device(): pl.pallas_call(functools.partial(kernel, S, V), out_shape=(jax.ShapeDtype...  52 us
    pallas_call x1, Pallas kernels, on_device(): pl.pallas_call(finish, out_shape=(jax.ShapeDtypeStruct((rows,), F32), jax...  1.74 us

profile of v1, /device:TPU:0, one launch (start us, length us, event | category | flops | bytes accessed | tf_op | source)
XLA Modules:
  0.0 54.4 jit_solution(17640660207062378397)
XLA Ops:
  0.6 52.0 %window_stats.1 = (f32[2,512]{1,0:T(2,128)}, s32[4,512]{1,0:T(4,128)}, f32[128,512]{1,0:T(8,128)}, s32[16,512]{1,0:T(8,128)}, f32[8,512]{1,0:T(8,128)}) custom-call(s32[512,4096]{1,0:T(8,128)} %gen_hbm.1, f32[1,4096]{1,0:T(1,128)} %bitcast.1), custom_call_target="tpu_custom_call" | custom-call | tf_op jit(solution)/shard_map/window_stats/pallas_call | solution.py:893
  52.7 1.7 %finish.1 = (f32[512]{0:T(512)}, f32[512]{0:T(512)}, s32[4,512]{1,0:T(4,128)}, f32[128,512]{1,0:T(8,128)}, s32[2,4096]{1,0:T(2,128)}, /*index=5*/f32[4096]{0:T(1024)}) custom-call(f32[2,512]{1,0:T(2,128)} %get-tuple-element.11.stats, s32[4,512]{1,0:T(4,128)} %get-tuple-element.12.counts, f32[128,512]{1,0:T(8,128)} %get-tuple-element.13.ld, ...), custom_call_target="tpu_custom_call" | custom-call | tf_op jit(solution)/shard_map/finish/pallas_call | solution.py:974

commit v2 on v1

--- a/solution.py
+++ b/solution.py
@@ -27,7 +27,7 @@
     S,
     V,
     gen_hbm,
-    w_ref,
+    w_hbm,
     stat_out,
     count_out,
     ld_out,
@@ -58,6 +58,7 @@
     qacc,
     root,
     gat,
+    tally,
     par,
     npar,
     ppar,
@@ -72,13 +73,17 @@
     smp_mine,
     smp_mate,
     smp_all,
+    w_ref,
     gen_sem,
+    w_sem,
     ncode_send,
     ncode_recv,
     pcode_send,
     pcode_recv,
     stat_send,
     stat_recv,
+    tally_send,
+    tally_recv,
     par_send,
     par_recv,
     yo_send,
@@ -105,6 +110,7 @@
     Q = H // 2
     PAIRS = S // 2
     NP = rows // SUB
+    GROUP = LANES // SUB
     UNIT = min(R, 64)
     NCP = rows // LANES
     KL = width * LEFT // 32 // LANES * LANES
@@ -133,6 +139,8 @@
     from_next = jnp.logical_or(next_part, next_full)
     from_prev = jnp.logical_or(send_up_full, send_up_part)
     does_prev = jnp.logical_or(prev_part, prev_full)
+    does_full = jnp.logical_or(next_full, prev_full)
+    hold = jnp.where(s == 0, 10, jnp.where(s < H, 5, 1))
     down = lax.rem(v + V - 1, V)
     up = lax.rem(v + 1, V)
     turn = lax.div(lax.div(pair * NP, PAIRS), 4) * 4
@@ -152,7 +160,10 @@
 
         lax.fori_loop(start, stop, step, 0)
 
-    loop(0, NP, lambda i: load(i).start())
+    w_load = pltpu.make_async_copy(w_hbm, w_ref, w_sem)
+    load(0).start()
+    w_load.start()
+    loop(1, NP, lambda i: load(i).start())
 
     barrier = pltpu.get_barrier_semaphore()
 
@@ -181,17 +192,17 @@
         + (PAIRS - 1) * (has_prev.astype(jnp.int32) + has_next.astype(jnp.int32))
     )
 
+    sacc[...] = jnp.zeros_like(sacc)
+    w_load.wait()
     root[...] = jnp.sqrt(w_ref[...])
-    sacc[...] = jnp.zeros_like(sacc)
-    qacc[...] = jnp.zeros_like(qacc)
 
     def piece_copy(i, buf, send, recv, device, lo, hi):
         here = piece_rows(i)
         return pltpu.make_async_remote_copy(
             src_ref=code.at[here, lo:hi],
             dst_ref=buf.at[here, lo:hi],
-            send_sem=send.at[i],
-            recv_sem=recv.at[i],
+            send_sem=send.at[lax.rem(i + turn, NP)],
+            recv_sem=recv.at[lax.rem(i + turn, NP)],
             device_id={"variants": device},
             device_id_type=MESH,
         )
@@ -210,6 +221,9 @@
         @pl.when(send_up_part)
         def _():
             up_copy(i, KL).start()
+
+    def total(x):
+        return jnp.sum(x.T, axis=0, keepdims=True)
 
     def first_pass(k):
         load(k).wait()
@@ -238,35 +252,39 @@
 
         loop(0, SUB // STEP, sixteen)
 
-        @pl.when(k == 0)
+        @pl.when(lax.rem(k, GROUP) == GROUP - 1)
+        def _():
+            group = pl.ds(aligned(base + SUB - LANES, LANES), LANES)
+            for i in range(3):
+                gat[s, i : i + 1, group] = total(wacc[i, group])
+            cnt = cacc[group]
+            for level in range(4):
+                some = jnp.bitwise_and(jnp.right_shift(cnt, 8 * level), 255)
+                tally[s, level : level + 1, group] = total(some.astype(F32))
+
+        def send(i):
+            @pl.when(send_down_full)
+            def _():
+                down_copy(i, width).start()
+
+            @pl.when(send_up_full)
+            def _():
+                up_copy(i, 0).start()
+
+            @pl.when(i < EARLY)
+            def _():
+                send_far(i)
+
+        @pl.when(k == hold)
         def _():
             pl.semaphore_wait(barrier, greetings)
-
-        @pl.when(send_down_full)
-        def _():
-            down_copy(k, width).start()
-
-        @pl.when(send_up_full)
-        def _():
-            up_copy(k, 0).start()
-
-        @pl.when(k < EARLY)
-        def _():
-            send_far(k)
+            loop(0, hold, send)
+
+        @pl.when(k >= hold)
+        def _():
+            send(k)
 
     loop(0, NP, first_pass)
-
-    def total(x):
-        return jnp.sum(x.T, axis=0, keepdims=True)
-
-    cnt = cacc[...]
-    lines = [total(wacc[i]) for i in range(3)]
-    for level in range(4):
-        lines.append(
-            total(jnp.bitwise_and(jnp.right_shift(cnt, 8 * level), 255).astype(F32))
-        )
-    lines.append(jnp.zeros_like(lines[0]))
-    gat[s] = jnp.concatenate(lines, axis=0)
 
     def stat_copy(d, slot):
         return pltpu.make_async_remote_copy(
@@ -274,6 +292,16 @@
             dst_ref=gat.at[slot],
             send_sem=stat_send.at[d],
             recv_sem=stat_recv.at[slot],
+            device_id={"samples": lax.rem(s + d, S)},
+            device_id_type=MESH,
+        )
+
+    def tally_copy(d, slot):
+        return pltpu.make_async_remote_copy(
+            src_ref=tally.at[slot],
+            dst_ref=tally.at[slot],
+            send_sem=tally_send.at[d],
+            recv_sem=tally_recv.at[slot],
             device_id={"samples": lax.rem(s + d, S)},
             device_id_type=MESH,
         )
@@ -321,7 +349,13 @@
     loop(EARLY, NP, send_far)
 
     stat_out[...] = jnp.concatenate([mean, var], axis=0)
-    count_out[...] = sums[3:7].astype(jnp.int32)
+    loop(1, S, lambda d: tally_copy(d, s).start())
+
+    def start_build(src, col):
+        aux[...] = jnp.concatenate([src[0:2], jnp.zeros((6, rows), F32)], axis=0)
+        turned = aux[...].T
+        for i in range(2):
+            col[i] = jnp.broadcast_to(turned[:, i : i + 1], (rows, LANES))
 
     def build(src, col, lane):
         def of(who):
@@ -333,15 +367,16 @@
         mine, its = of(s), of(mate)
         both = jnp.sqrt(mine * mine + its * its)
         aux[...] = jnp.concatenate(
-            [src[0:2], FULL / mine, its, FULL / both, jnp.zeros((3, rows), F32)],
-            axis=0,
+            [FULL / mine, its, FULL / both, jnp.zeros((5, rows), F32)], axis=0
         )
         turned = aux[...].T
-        for i in range(5):
-            col[i] = jnp.broadcast_to(turned[:, i : i + 1], (rows, LANES))
+        for i in range(3):
+            col[2 + i] = jnp.broadcast_to(turned[:, i : i + 1], (rows, LANES))
         lane[0:1] = 1.0 / mine
         lane[1:2] = its * (1.0 / FULL)
         lane[2:3] = 1.0 / both
+
+    def build_tall(src):
         sizes = []
         for q in range(PAIRS):
             a, b = src[2 + 2 * q : 3 + 2 * q], src[3 + 2 * q : 4 + 2 * q]
@@ -351,7 +386,7 @@
             sizes.append(jnp.zeros((left, rows), F32))
         tall[:, 0 : PAIRS + left] = jnp.concatenate(sizes, axis=0).T
 
-    def scale(src, src_row, dst, dst_row, count, lo, hi, col, squares):
+    def scale(src, src_row, dst, dst_row, count, lo, hi, col):
         def sixteen(i):
             here = pl.ds(aligned(src_row + i * STEP, STEP), STEP)
             there = pl.ds(aligned(dst_row + i * STEP, STEP), STEP)
@@ -362,10 +397,6 @@
                 r = jnp.broadcast_to(root[0:1, lane], (STEP, LANES))
                 x = jnp.where(d < 2.5, r * (d - m) * f, 0.0).astype(BF16)
                 dst[there, lane] = x
-                if squares:
-                    yy = x.astype(F32)
-                    yy = yy * yy
-                    qacc[:, lane] += yy[:8] + yy[8:]
 
         loop(0, count // STEP, sixteen)
 
@@ -376,17 +407,9 @@
                 tall[pl.ds(aligned(row, R), R), q : q + 1], (R, LANES)
             )
 
+    start_build(par, col_o)
+    scale(code, 0, scaled, 0, rows, 0, width, col_o)
     build(par, col_o, lane_o)
-    for q in range(PAIRS):
-        lane_q[q] = jnp.sqrt(
-            par[2 + 2 * q : 3 + 2 * q] ** 2 + par[3 + 2 * q : 4 + 2 * q] ** 2
-        ) * (1.0 / FULL)
-
-    @pl.when(s < H)
-    def _():
-        rows_of()
-
-    scale(code, 0, scaled, 0, rows, 0, width, col_o, True)
 
     def dot(a, b):
         return lax.dot_general(
@@ -468,35 +491,23 @@
             {"samples": 2 * j + y},
         )
 
-    def own_dot(o):
-        here = pl.ds(aligned(o * R, R), R)
+    TALL = min(rows, 256)
+    PER = TALL // R
+
+    def own_rows(k):
+        first = lax.rem(k * TALL + lax.div(turn * SUB, TALL) * TALL, rows)
+        here = pl.ds(aligned(first, TALL), TALL)
         keep_o[here, :] = dot(scaled[here, :], scaled[...])
 
-    def own_rows(k):
-        give = k < Q
-        j = lax.rem(lax.rem(k, Q) + pair, Q)
-        o = 2 * j + jnp.where(give, 1 - y, y)
-        own_dot(o)
-
-        @pl.when(give)
-        def _():
-            pack(
-                keep_o, o * R, col_o, o * R, lane_o, 0, rows, R, ypart_o.at[j], 0
-            )
+        def give(i):
+            o = lax.div(first, R) + 2 * i + 1 - y
+            j = lax.div(o, 2)
+            pack(keep_o, o * R, col_o, o * R, lane_o, 0, rows, R, ypart_o.at[j], 0)
             yo_copy(j).start()
 
-    loop(0, H, own_rows)
-
-    packed = sacc[...]
-    tags = [
-        jnp.bitwise_and(jnp.right_shift(packed, 8 * level), 255).astype(F32)
-        for level in range(3)
-    ]
-    for q, value in enumerate([tags[0] + tags[1] + tags[2], tags[1], qacc[...]]):
-        line = jnp.sum(value, axis=0, keepdims=True)
-        for i in range(slabs):
-            at = q * slabs + i
-            smp_mine[at : at + 1, :] = line[:, i * SLAB : (i + 1) * SLAB]
+        loop(0, PER // 2, give)
+
+    loop(0, rows // TALL, own_rows)
 
     mate_copy = copy_to(
         smp_mine,
@@ -505,10 +516,65 @@
         mate_recv.at[0],
         {"variants": v + 1 - 2 * (v - 2 * chip)},
     )
-    mate_copy.start()
+    def squares(b):
+        lanes = pl.ds(aligned(b * LANES, LANES), LANES)
+        sums = [jnp.zeros((8, LANES), F32) for _ in range(4)]
+        for i in range(rows // STEP):
+            x = scaled[i * STEP : (i + 1) * STEP, lanes].astype(F32)
+            x = x * x
+            k = 2 * (i % 2)
+            sums[k] = sums[k] + x[:8]
+            sums[k + 1] = sums[k + 1] + x[8:]
+        qacc[:, lanes] = (sums[0] + sums[1]) + (sums[2] + sums[3])
+
+    def sample_sums():
+        loop(0, blocks, squares)
+        packed = sacc[...]
+        tags = [
+            jnp.bitwise_and(jnp.right_shift(packed, 8 * level), 255).astype(F32)
+            for level in range(3)
+        ]
+        for q, value in enumerate([tags[0] + tags[1] + tags[2], tags[1], qacc[...]]):
+            line = jnp.sum(value, axis=0, keepdims=True)
+            for i in range(slabs):
+                at = q * slabs + i
+                smp_mine[at : at + 1, :] = line[:, i * SLAB : (i + 1) * SLAB]
+        mate_copy.start()
+
+
+    def smp_copy(d, slot):
+        return copy_to(
+            smp_all.at[slot],
+            smp_all.at[slot],
+            smp_send.at[d],
+            smp_recv.at[slot],
+            {"variants": lax.rem(v + 2 * d, V)},
+        )
+
+    def share_sums():
+        mate_copy.wait_recv()
+        smp_all[chip] = smp_mine[...] + smp_mate[...]
+        loop(1, C, lambda d: smp_copy(d, chip).start())
+
+    def own_norms():
+        for q in range(PAIRS):
+            a, b = par[2 + 2 * q : 3 + 2 * q], par[3 + 2 * q : 4 + 2 * q]
+            lane_q[q] = jnp.sqrt(a * a + b * b) * (1.0 / FULL)
+
+        @pl.when(s < H)
+        def _():
+            build_tall(par)
+            rows_of()
+
+    def rows_of():
+        row = lax.rem(s, H) * R
+        for q in range(PAIRS):
+            spread[q] = jnp.broadcast_to(
+                tall[pl.ds(aligned(row, R), R), q : q + 1], (R, LANES)
+            )
 
     def collect_own(k):
-        j = lax.rem(k + pair, Q)
+        j = lax.rem(k + lax.div(turn * SUB, TALL) * (PER // 2), Q)
         o = 2 * j + y
         yo_copy(j).wait_recv()
         args = (keep_o, o * R, yrcv_o.at[j], 0, col_o, o * R, lane_o, 0, rows, R)
@@ -546,14 +612,13 @@
         )
 
     def next_rows(k, size):
-        return lax.rem(k * size + turn * SUB, rows)
+        return lax.rem(k * size + lax.div(turn * SUB, size) * size, rows)
 
     def next_parity(at):
         r = lax.div(at, R)
         return r - 2 * lax.div(r, 2) == y
 
-    def collect_next(k, size):
-        at = next_rows(k, size)
+    def collect_next(at, size):
         r = lax.div(at, R)
 
         @pl.when(next_parity(at))
@@ -572,40 +637,91 @@
                 merge(*args, zpart_n.at[j], off, False)
                 zn_copy(at, size).start()
 
-    def next_role(size, hi):
-        per = size // SUB
+    def give_next(at, size):
+        r = lax.div(at, R)
+
+        @pl.when(jnp.logical_not(next_parity(at)))
+        def _():
+            j = lax.div(r, 2)
+            pack(
+                keep_x, at, col_x, at, lane_o, 0, rows, size, ypart_n.at[j], at - r * R
+            )
+            yn_copy(at, size).start()
+
+    def next_dot(at, tall_rows, hi):
+        def arrived(i):
+            down_copy(lax.rem(lax.div(at, SUB) + i + NP - turn, NP), hi).wait_recv()
+
+        loop(0, tall_rows // SUB, arrived)
+        scale(ncode, at, other, 0, tall_rows, 0, hi, col_x)
+        here = pl.ds(aligned(at, tall_rows), tall_rows)
+        keep_x[here, :] = dot(other[0:tall_rows, 0:hi], scaled[:, 0:hi])
+
+    def next_role_full():
+        pieces = TALL // R
+
+        def each(at, act):
+            loop(0, pieces, lambda i: act(at + i * R, R))
+
+        count = rows // TALL
+        for k in range(count):
+            at = next_rows(k, TALL)
+            next_dot(at, TALL, width)
+            each(at, give_next)
+            if k == 0:
+                sample_sums()
+                loop(0, Q, collect_own)
+            else:
+                each(next_rows(k - 1, TALL), collect_next)
+        share_sums()
+        own_norms()
+        each(next_rows(count - 1, TALL), collect_next)
+        next_norms()
+
+    def next_role_part(hi):
+        wide = LANES // UNIT
+        count = rows // LANES
+
+        def each(at, act):
+            loop(0, wide, lambda i: act(at + i * UNIT, UNIT))
+
+        def middle():
+            sample_sums()
+            loop(0, Q, collect_own)
+            share_sums()
+            own_norms()
 
         def chunk(k):
-            at = next_rows(k, size)
-            for i in range(per):
-                down_copy(k * per + i, hi).wait_recv()
-            scale(ncode, at, other, 0, size, 0, hi, col_x, False)
-            here = pl.ds(aligned(at, size), size)
-            keep_x[here, :] = dot(other[0:size, 0:hi], scaled[:, 0:hi])
-            r = lax.div(at, R)
-
-            @pl.when(jnp.logical_not(next_parity(at)))
+            at = next_rows(k, LANES)
+            next_dot(at, LANES, hi)
+            each(at, give_next)
+
+            @pl.when(jnp.logical_and(k == 1, jnp.logical_not(does_full)))
             def _():
-                pack(
-                    keep_x,
-                    at,
-                    col_x,
-                    at,
-                    lane_o,
-                    0,
-                    rows,
-                    size,
-                    ypart_n.at[lax.div(r, 2)],
-                    at - r * R,
-                )
-                yn_copy(at, size).start()
+                middle()
 
             @pl.when(k > 0)
             def _():
-                collect_next(k - 1, size)
-
-        loop(0, rows // size, chunk)
-        collect_next(rows // size - 1, size)
+                each(next_rows(k - 1, LANES), collect_next)
+
+        loop(0, count - 1, chunk)
+        next_norms()
+
+        def small(k):
+            at = next_rows(count - 1, LANES) + k * UNIT
+            next_dot(at, UNIT, hi)
+            give_next(at, UNIT)
+
+            @pl.when(k == 0)
+            def _():
+                each(next_rows(count - 2, LANES), collect_next)
+
+            @pl.when(k > 0)
+            def _():
+                collect_next(at - UNIT, UNIT)
+
+        loop(0, wide, small)
+        collect_next(next_rows(count - 1, LANES) + LANES - UNIT, UNIT)
 
     def yp_copy(c):
         return copy_to(
@@ -621,11 +737,7 @@
             {"samples": H + 2 * j + y, "variants": down},
         )
 
-    def prev_chunk(k):
-        return lax.rem(k + lax.div(turn * SUB, LANES), NCP)
-
-    def collect_prev(k):
-        c = prev_chunk(k)
+    def collect_prev(c):
         yp_copy(c).wait_recv()
 
         def one(i):
@@ -650,94 +762,124 @@
 
         loop(0, Q, one)
 
-    def prev_role(lo):
-        per = LANES // SUB
+    def prev_dot(c, wide, lo):
+        def arrived(i):
+            up_copy(lax.rem(c * GROUP + i + NP - turn, NP), lo).wait_recv()
+
+        loop(0, wide * GROUP, arrived)
+        scale(pcode, c * LANES, other, 0, wide * LANES, lo, width, col_x)
+        got = dot(scaled[:, lo:width], other[0 : wide * LANES, lo:width])
+        for i in range(wide):
+            here = pl.ds(aligned((c + i) * rows, rows), rows)
+            keep_x[here, 0:LANES] = got[:, i * LANES : (i + 1) * LANES]
+
+    def give_prev(c):
+        def one(j):
+            o = (2 * j + 1 - y) * R
+            pack(
+                keep_x,
+                c * rows + o,
+                col_o,
+                o,
+                lane_x,
+                c * LANES,
+                LANES,
+                R,
+                ypart_p.at[c, j],
+                0,
+            )
+
+        loop(0, Q, one)
+        yp_copy(c).start()
+
+    def prev_role(wide, lo, full):
+        count = NCP // wide
+        first = lax.div(lax.div(turn, GROUP), wide)
+
+        def at(k):
+            return lax.rem(k + first, count) * wide
+
+        def each(k, act):
+            loop(0, wide, lambda i: act(at(k) + i))
 
         def chunk(k):
-            c = prev_chunk(k)
-            for i in range(per):
-                up_copy(k * per + i, lo).wait_recv()
-            scale(pcode, c * LANES, other, 0, LANES, lo, width, col_x, False)
-            here = pl.ds(aligned(c * rows, rows), rows)
-            keep_x[here, 0:LANES] = dot(scaled[:, lo:width], other[0:LANES, lo:width])
-
-            def one(j):
-                o = (2 * j + 1 - y) * R
-                pack(
-                    keep_x,
-                    c * rows + o,
-                    col_o,
-                    o,
-                    lane_x,
-                    c * LANES,
-                    LANES,
-                    R,
-                    ypart_p.at[c, j],
-                    0,
-                )
-
-            loop(0, Q, one)
-            yp_copy(c).start()
-
-            @pl.when(k > 0)
+            prev_dot(at(k), wide, lo)
+            each(k, give_prev)
+
+        def middle():
+            sample_sums()
+            loop(0, Q, collect_own)
+            share_sums()
+            own_norms()
+
+        if full:
+            chunk(0)
+            middle()
+        else:
+            chunk(0)
+            chunk(1)
+
+            @pl.when(jnp.logical_not(does_full))
             def _():
-                collect_prev(k - 1)
-
-        loop(0, NCP, chunk)
-        collect_prev(NCP - 1)
+                middle()
+
+            each(0, collect_prev)
+
+        def rest(k):
+            chunk(k)
+            each(k - 1, collect_prev)
+
+        loop(1 if full else 2, count, rest)
+        each(count - 1, collect_prev)
 
     def with_next():
         par_copy(0, npar, down).wait_recv()
+        start_build(npar, col_x)
         build(npar, col_x, lane_x)
 
+    def next_norms():
         @pl.when(s >= H)
         def _():
+            build_tall(npar)
             rows_of()
 
 
     def with_prev():
         par_copy(1, ppar, up).wait_recv()
+        start_build(ppar, col_x)
         build(ppar, col_x, lane_x)
 
+
     @pl.when(prev_full)
     def _():
         with_prev()
-        prev_role(0)
+        prev_role(min(2, NCP), 0, True)
 
     @pl.when(next_full)
     def _():
         with_next()
-        next_role(R, width)
-
-    loop(0, Q, collect_own)
-
-    mate_copy.wait_recv()
-    smp_all[chip] = smp_mine[...] + smp_mate[...]
-
-    def smp_copy(d, slot):
-        return copy_to(
-            smp_all.at[slot],
-            smp_all.at[slot],
-            smp_send.at[d],
-            smp_recv.at[slot],
-            {"variants": lax.rem(v + 2 * d, V)},
-        )
-
-    loop(1, C, lambda d: smp_copy(d, chip).start())
+        next_role_full()
 
     @pl.when(prev_part)
     def _():
         with_prev()
-        prev_role(KL)
+        prev_role(1, KL, False)
 
     @pl.when(next_part)
     def _():
         with_next()
-        next_role(UNIT, KL)
+        next_role_part(KL)
 
     @pl.when(jnp.logical_and(jnp.logical_not(from_next), has_next))
     def _():
-        with_next()
+        par_copy(0, npar, down).wait_recv()
+        next_norms()
+
+    loop(1, S, lambda d: tally_copy(d, lax.rem(s + d, S)).wait_recv())
+    counts = tally[0]
+    for t in range(1, S):
+        counts = counts + tally[t]
+    count_out[...] = counts.astype(jnp.int32)
 
     loop(1, C, lambda d: smp_copy(d, lax.rem(chip + d, C)).wait_recv())
     all_sums = smp_all[0]
@@ -791,6 +933,7 @@
             loop(0, PAIRS, gather_prev)
 
     loop(1, S, lambda d: stat_copy(d, s).wait_send())
+    loop(1, S, lambda d: tally_copy(d, s).wait_send())
     loop(1, C, lambda d: smp_copy(d, chip).wait_send())
     mate_copy.wait_send()
 
@@ -805,15 +948,14 @@
 
     def drain_next(size):
         def one(k):
-            at = next_rows(k, size)
-            r = lax.div(at, R)
+            at = k * size
             mine = next_parity(at)
 
             @pl.when(jnp.logical_not(mine))
             def _():
                 yn_copy(at, size).wait_send()
 
-            @pl.when(jnp.logical_and(mine, H + r != s))
+            @pl.when(jnp.logical_and(mine, H + lax.div(at, R) != s))
             def _():
                 zn_copy(at, size).wait_send()
 
@@ -899,7 +1041,7 @@
             jax.ShapeDtypeStruct((2 * slabs, SLAB), jnp.int32),
             jax.ShapeDtypeStruct((slabs, SLAB), F32),
         ),
-        in_specs=[pl.BlockSpec(memory_space=pl.ANY), vmem],
+        in_specs=[pl.BlockSpec(memory_space=pl.ANY)] * 2,
         out_specs=(vmem,) * 5,
         scratch_shapes=[
             pltpu.VMEM((rows, width), jnp.int32),
@@ -907,7 +1049,7 @@
             pltpu.VMEM((rows, width), BF16),
             pltpu.VMEM((rows, width), BF16),
             pltpu.VMEM((rows, width), BF16),
-            pltpu.VMEM((max(R, LANES), width), BF16),
+            pltpu.VMEM((min(rows, 256), width), BF16),
             pltpu.VMEM((rows, rows), F32),
             pltpu.VMEM((NCP * rows, rows), F32),
             pltpu.VMEM((Q, R, rows), jnp.int16),
@@ -926,7 +1068,8 @@
             pltpu.VMEM((8, width), jnp.int32),
             pltpu.VMEM((8, width), F32),
             pltpu.VMEM((1, width), F32),
-            pltpu.VMEM((S, 8, rows), F32),
+            pltpu.VMEM((S, 3, rows), F32),
+            pltpu.VMEM((S, 4, rows), F32),
             pltpu.VMEM((lines, rows), F32),
             pltpu.VMEM((lines, rows), F32),
             pltpu.VMEM((lines, rows), F32),
@@ -941,11 +1084,15 @@
             pltpu.VMEM((3 * slabs, SLAB), F32),
             pltpu.VMEM((3 * slabs, SLAB), F32),
             pltpu.VMEM((C, 3 * slabs, SLAB), F32),
+            pltpu.VMEM((1, width), F32),
+            dma((NP,)),
+            dma(()),
             dma((NP,)),
             dma((NP,)),
             dma((NP,)),
             dma((NP,)),
-            dma((NP,)),
+            dma((S,)),
+            dma((S,)),
             dma((S,)),
             dma((S,)),
             dma((2,)),

time: 54.6 us -> 44.9 us (0.82)
  the two profiles are of different devices: /device:TPU:0 before, /device:TPU:21 now
where the time goes in v2:
time: 44.9 us; the launch traced here: 44.2 us
  Pallas kernels  43.5 us (97%)
  between operations  0.64 us (1%)
    pallas_call x1, Pallas kernels, on_device(): pl.pallas_call(functools.partial(kernel, S, V), out_shape=(jax.ShapeDtype...  41.8 us
    pallas_call x1, Pallas kernels, on_device(): pl.pallas_call(finish, out_shape=(jax.ShapeDtypeStruct((rows,), F32), jax...  1.74 us

profile of v2, /device:TPU:21, one launch (start us, length us, event | category | flops | bytes accessed | tf_op | source)
XLA Modules:
  0.0 44.2 jit_solution(4930245443945507976)
XLA Ops:
  0.6 41.8 %window_stats.1 = (f32[2,512]{1,0:T(2,128)}, s32[4,512]{1,0:T(4,128)}, f32[128,512]{1,0:T(8,128)}, s32[16,512]{1,0:T(8,128)}, f32[8,512]{1,0:T(8,128)}) custom-call(s32[512,4096]{1,0:T(8,128)} %gen_hbm.1, f32[1,4096]{1,0:T(1,128)} %bitcast.1), custom_call_target="tpu_custom_call" | custom-call | tf_op jit(solution)/shard_map/window_stats/pallas_call | solution.py:1035
  42.4 1.7 %finish.1 = (f32[512]{0:T(512)}, f32[512]{0:T(512)}, s32[4,512]{1,0:T(4,128)}, f32[128,512]{1,0:T(8,128)}, s32[2,4096]{1,0:T(2,128)}, /*index=5*/f32[4096]{0:T(1024)}) custom-call(f32[2,512]{1,0:T(2,128)} %get-tuple-element.11.stats, s32[4,512]{1,0:T(4,128)} %get-tuple-element.12.counts, f32[128,512]{1,0:T(8,128)} %get-tuple-element.13.ld, ...), custom_call_target="tpu_custom_call" | custom-call | tf_op jit(solution)/shard_map/finish/pallas_call | solution.py:1121

commit v3 on v2

--- a/solution.py
+++ b/solution.py
@@ -573,6 +573,9 @@
                 tall[pl.ds(aligned(row, R), R), q : q + 1], (R, LANES)
             )
 
+    def own_half(i):
+        loop(i * (Q // 2), (i + 1) * (Q // 2), collect_own)
+
     def collect_own(k):
         j = lax.rem(k + lax.div(turn * SUB, TALL) * (PER // 2), Q)
         o = 2 * j + y
@@ -669,13 +672,15 @@
             next_dot(at, TALL, width)
             each(at, give_next)
             if k == 0:
-                sample_sums()
-                loop(0, Q, collect_own)
-            else:
+                own_half(0)
+            if k == count - 1:
+                own_half(1)
+            if k > 0:
                 each(next_rows(k - 1, TALL), collect_next)
+        sample_sums()
+        each(next_rows(count - 1, TALL), collect_next)
         share_sums()
         own_norms()
-        each(next_rows(count - 1, TALL), collect_next)
         next_norms()
 
     def next_role_part(hi):
@@ -685,20 +690,21 @@
         def each(at, act):
             loop(0, wide, lambda i: act(at + i * UNIT, UNIT))
 
-        def middle():
-            sample_sums()
-            loop(0, Q, collect_own)
-            share_sums()
-            own_norms()
+        alone = jnp.logical_not(does_full)
 
         def chunk(k):
             at = next_rows(k, LANES)
             next_dot(at, LANES, hi)
             each(at, give_next)
 
-            @pl.when(jnp.logical_and(k == 1, jnp.logical_not(does_full)))
-            def _():
-                middle()
+            @pl.when(jnp.logical_and(k == 0, alone))
+            def _():
+                own_half(0)
+
+            @pl.when(jnp.logical_and(k == 1, alone))
+            def _():
+                sample_sums()
+                own_half(1)
 
             @pl.when(k > 0)
             def _():
@@ -721,6 +727,12 @@
                 collect_next(at - UNIT, UNIT)
 
         loop(0, wide, small)
+
+        @pl.when(alone)
+        def _():
+            share_sums()
+            own_norms()
+
         collect_next(next_rows(count - 1, LANES) + LANES - UNIT, UNIT)
 
     def yp_copy(c):
@@ -806,30 +818,44 @@
             prev_dot(at(k), wide, lo)
             each(k, give_prev)
 
-        def middle():
-            sample_sums()
-            loop(0, Q, collect_own)
-            share_sums()
-            own_norms()
-
         if full:
             chunk(0)
-            middle()
+            own_half(0)
+            chunk(1)
+            own_half(1)
+            each(0, collect_prev)
+            sample_sums()
         else:
+            alone = jnp.logical_not(does_full)
             chunk(0)
+
+            @pl.when(alone)
+            def _():
+                own_half(0)
+
             chunk(1)
 
-            @pl.when(jnp.logical_not(does_full))
-            def _():
-                middle()
+            @pl.when(alone)
+            def _():
+                own_half(1)
 
             each(0, collect_prev)
+
+            @pl.when(alone)
+            def _():
+                sample_sums()
 
         def rest(k):
             chunk(k)
             each(k - 1, collect_prev)
 
-        loop(1 if full else 2, count, rest)
+        loop(2, count, rest)
+
+        @pl.when(jnp.logical_or(full, jnp.logical_not(does_full)))
+        def _():
+            share_sums()
+            own_norms()
+
         each(count - 1, collect_prev)
 
     def with_next():
@@ -874,6 +900,35 @@
     def _():
         par_copy(0, npar, down).wait_recv()
         next_norms()
+
+    loop(1, S, lambda d: stat_copy(d, s).wait_send())
+    loop(1, S, lambda d: tally_copy(d, s).wait_send())
+    mate_copy.wait_send()
+
+
+    @pl.when(has_prev)
+    def _():
+        par_copy(0, npar, down).wait_send()
+
+    @pl.when(from_prev)
+    def _():
+        par_copy(1, ppar, up).wait_send()
+
+    @pl.when(send_down_full)
+    def _():
+        loop(0, NP, lambda i: down_copy(i, width).wait_send())
+
+    @pl.when(send_down_part)
+    def _():
+        loop(0, NP, lambda i: down_copy(i, KL).wait_send())
+
+    @pl.when(send_up_full)
+    def _():
+        loop(0, NP, lambda i: up_copy(i, 0).wait_send())
+
+    @pl.when(send_up_part)
+    def _():
+        loop(0, NP, lambda i: up_copy(i, KL).wait_send())
 
     loop(1, S, lambda d: tally_copy(d, lax.rem(s + d, S)).wait_recv())
     counts = tally[0]
@@ -932,11 +987,6 @@
         def _():
             loop(0, PAIRS, gather_prev)
 
-    loop(1, S, lambda d: stat_copy(d, s).wait_send())
-    loop(1, S, lambda d: tally_copy(d, s).wait_send())
-    loop(1, C, lambda d: smp_copy(d, chip).wait_send())
-    mate_copy.wait_send()
-
     def drain_own(j):
         yo_copy(j).wait_send()
 
@@ -980,29 +1030,7 @@
 
         loop(0, Q, drain)
 
-    @pl.when(has_prev)
-    def _():
-        par_copy(0, npar, down).wait_send()
-
-    @pl.when(from_prev)
-    def _():
-        par_copy(1, ppar, up).wait_send()
-
-    @pl.when(send_down_full)
-    def _():
-        loop(0, NP, lambda i: down_copy(i, width).wait_send())
-
-    @pl.when(send_down_part)
-    def _():
-        loop(0, NP, lambda i: down_copy(i, KL).wait_send())
-
-    @pl.when(send_up_full)
-    def _():
-        loop(0, NP, lambda i: up_copy(i, 0).wait_send())
-
-    @pl.when(send_up_part)
-    def _():
-        loop(0, NP, lambda i: up_copy(i, KL).wait_send())
+    loop(1, C, lambda d: smp_copy(d, chip).wait_send())
 
 
 def finish(stats, counts, ld, calls, share, mean, var, counts_o, ld_o, calls_o, share_o):
@@ -1032,14 +1060,14 @@
     slabs = width // SLAB
     vmem = pl.BlockSpec(memory_space=pltpu.VMEM)
     dma = pltpu.SemaphoreType.DMA
-    stats, counts, ld, calls, share = pl.pallas_call(
+    results = pl.pallas_call(
         functools.partial(kernel, S, V),
         out_shape=(
-            jax.ShapeDtypeStruct((2, rows), F32),
-            jax.ShapeDtypeStruct((4, rows), jnp.int32),
-            jax.ShapeDtypeStruct((R, rows), F32),
-            jax.ShapeDtypeStruct((2 * slabs, SLAB), jnp.int32),
-            jax.ShapeDtypeStruct((slabs, SLAB), F32),
+            pltpu.VMEM((2, rows), F32),
+            pltpu.VMEM((4, rows), jnp.int32),
+            pltpu.VMEM((R, rows), F32),
+            pltpu.VMEM((2 * slabs, SLAB), jnp.int32),
+            pltpu.VMEM((slabs, SLAB), F32),
         ),
         in_specs=[pl.BlockSpec(memory_space=pl.ANY)] * 2,
         out_specs=(vmem,) * 5,
@@ -1118,6 +1146,7 @@
         ),
         name="window_stats",
     )(genotypes, weights.reshape(1, width))
+    results = [pltpu.with_memory_space_constraint(x, pltpu.VMEM) for x in results]
     return pl.pallas_call(
         finish,
         out_shape=(
@@ -1131,7 +1160,7 @@
         in_specs=[vmem] * 5,
         out_specs=(vmem,) * 6,
         name="finish",
-    )(stats, counts, ld, calls, share)
+    )(*results)
 
 
 def solution(mesh):

time: 44.9 us -> 42.2 us (0.940)
  Pallas kernels: 43.5 us -> 41 us
    pallas_call x1, Pallas kernels: 41.8 us -> 40.3 us  [on_device(): pl.pallas_call(functools.partial(kernel, S, V), out_shape=(pltpu.VMEM((2,...]
    pallas_call x1, Pallas kernels: 1.74 us -> 0.75 us  [on_device(): pl.pallas_call(finish, out_shape=(jax.ShapeDtypeStruct((rows,), F32), jax...]
where the time goes in v3:
time: 42.2 us; the launch traced here: 41.7 us
  Pallas kernels  41 us (97%)
  between operations  0.64 us (2%)
    pallas_call x1, Pallas kernels, on_device(): pl.pallas_call(functools.partial(kernel, S, V), out_shape=(pltpu.VMEM((2,...  40.3 us

profile of v3, /device:TPU:21, one launch (start us, length us, event | category | flops | bytes accessed | tf_op | source)
XLA Modules:
  0.0 41.7 jit_solution(13833674149710286164)
XLA Ops:
  0.6 40.3 %window_stats.1 = (f32[2,512]{1,0:T(2,128)S(1)}, s32[4,512]{1,0:T(4,128)S(1)}, f32[128,512]{1,0:T(8,128)S(1)}, s32[16,512]{1,0:T(8,128)S(1)}, f32[8,512]{1,0:T(8,128)S(1)}) custom-call(s32[512,4096]{1,0:T(8,128)} %gen_hbm.1, f32[1,4096]{1,0:T(1,128)} %bitcast.1), custom_call_target="tpu_custom_call" | custom-call | tf_op jit(solution)/shard_map/window_stats/pallas_call | solution.py:1063
  40.9 0.7 %finish.1 = (f32[512]{0:T(512)}, f32[512]{0:T(512)}, s32[4,512]{1,0:T(4,128)}, f32[128,512]{1,0:T(8,128)}, s32[2,4096]{1,0:T(2,128)}, /*index=5*/f32[4096]{0:T(1024)}) custom-call(f32[2,512]{1,0:T(2,128)S(1)} %get-tuple-element.11.stats, s32[4,512]{1,0:T(4,128)S(1)} %get-tuple-element.12.counts, f32[128,512]{1,0:T(8,128)S(1)} %get-tuple-element.13.ld, ...), custom_call_target="tpu_custom_call" | custom-call | tf_op jit(solution)/shard_map/finish/pallas_call | solution.py:1150

commit v4 on v3

--- a/solution.py
+++ b/solution.py
@@ -140,7 +140,7 @@
     from_prev = jnp.logical_or(send_up_full, send_up_part)
     does_prev = jnp.logical_or(prev_part, prev_full)
     does_full = jnp.logical_or(next_full, prev_full)
-    hold = jnp.where(s == 0, 10, jnp.where(s < H, 5, 1))
+    hold = jnp.where(s == 0, 12, jnp.where(s < H, 7, 3))
     down = lax.rem(v + V - 1, V)
     up = lax.rem(v + 1, V)
     turn = lax.div(lax.div(pair * NP, PAIRS), 4) * 4

time: 42.2 us -> 42.1 us (level)
  no operation moved by 1% of the time
where the time goes in v4:
time: 42.1 us; the launch traced here: 41.7 us
  Pallas kernels  41.1 us (98%)
  between operations  0.64 us (2%)
    pallas_call x1, Pallas kernels, on_device(): pl.pallas_call(functools.partial(kernel, S, V), out_shape=(pltpu.VMEM((2,...  40.3 us

profile of v4, /device:TPU:21, one launch (start us, length us, event | category | flops | bytes accessed | tf_op | source)
XLA Modules:
  0.0 41.7 jit_solution(13139337146685971051)
XLA Ops:
  0.6 40.3 %window_stats.1 = (f32[2,512]{1,0:T(2,128)S(1)}, s32[4,512]{1,0:T(4,128)S(1)}, f32[128,512]{1,0:T(8,128)S(1)}, s32[16,512]{1,0:T(8,128)S(1)}, f32[8,512]{1,0:T(8,128)S(1)}) custom-call(s32[512,4096]{1,0:T(8,128)} %gen_hbm.1, f32[1,4096]{1,0:T(1,128)} %bitcast.1), custom_call_target="tpu_custom_call" | custom-call | tf_op jit(solution)/shard_map/window_stats/pallas_call | solution.py:1063
  41.0 0.7 %finish.1 = (f32[512]{0:T(512)}, f32[512]{0:T(512)}, s32[4,512]{1,0:T(4,128)}, f32[128,512]{1,0:T(8,128)}, s32[2,4096]{1,0:T(2,128)}, /*index=5*/f32[4096]{0:T(1024)}) custom-call(f32[2,512]{1,0:T(2,128)S(1)} %get-tuple-element.11.stats, s32[4,512]{1,0:T(4,128)S(1)} %get-tuple-element.12.counts, f32[128,512]{1,0:T(8,128)S(1)} %get-tuple-element.13.ld, ...), custom_call_target="tpu_custom_call" | custom-call | tf_op jit(solution)/shard_map/finish/pallas_call | solution.py:1150
